TPU v7x, 32 devices: a whole 2x2x4 slice. The times are simulated.
32 devices in a mesh: grp: 8 (over z, x), vocab: 4 (over y, core).
Axes of the slice: x: 2, y: 2, z: 4, core: 2. Of those that a mesh axis runs over, the one named last changes fastest.
Arguments:
- teacher_rows: bfloat16 [64, 8, 4096], P('grp', None, 'vocab'), may hold values from -160 to 160
- student_rows: bfloat16 [8, 32, 5120], P('grp', None, 'vocab'), may hold values from -160 to 160
- teacher_head: bfloat16 [4096, 8192], P(None, ('grp', 'vocab')), may hold values from -0.25 to 0.25
- student_head: bfloat16 [5120, 8192], P(None, ('grp', 'vocab')), may hold values from -0.25 to 0.25
- lengths: int32 [64], replicated, may hold values from 1 to 8, as said below
- owner: int32 [64], replicated, may hold values from 0 to 7, as said below
Outputs:
- divergence: float32 [8, 32], P('grp')
- grad_student: bfloat16 [8, 32, 5120], P('grp', None, 'vocab')
Inputs may be any that keep to these rules, and one draw needn't show every extreme that they name: All 8 sequences of one teacher group share one owner, and each student group owns the sequences of exactly one teacher group. The lengths of the 8 sequences of one teacher group sum to at most 32, and to exactly 32 for some group.
All inputs are finite; a program needn't handle non-finite values.
Results may differ from a plain program's by a relative error of at most 0.018.
Values may be sent and summed in bfloat16 or wider, within the bound.
A program may use at most 64 MiB of HBM per device.

v0:
```python
import jax
import jax.numpy as jnp
from jax import lax
from jax.sharding import PartitionSpec as P


def routing_tables(lengths, owner, groups, seq_count, positions, pad_rows):
    slot_count = seq_count * positions
    group_ids = jnp.arange(groups, dtype=jnp.int32)
    length_table = lengths.reshape(groups, seq_count)
    owner_table = owner.reshape(groups, seq_count)[:, 0]
    teacher_of = jnp.sum(
        (owner_table[None, :] == group_ids[:, None]).astype(jnp.int32) * group_ids[None, :], axis=1
    )
    position_ids = jnp.arange(positions, dtype=jnp.int32)
    live_slots = (position_ids[None, None, :] < length_table[:, :, None]).reshape(
        groups, slot_count
    )
    ranked = jnp.cumsum(live_slots.astype(jnp.int32), axis=1) - 1
    target = jnp.where(live_slots, ranked, pad_rows)
    matches = target[:, None, :] == jnp.arange(pad_rows, dtype=jnp.int32)[None, :, None]
    source = jnp.sum(
        matches.astype(jnp.int32) * jnp.arange(slot_count, dtype=jnp.int32)[None, None, :], axis=2
    )
    totals = jnp.sum(length_table, axis=1)
    owned_total = jnp.take(totals, teacher_of, axis=0)
    student_live = jnp.arange(pad_rows, dtype=jnp.int32)[None, :] < owned_total[:, None]
    return (teacher_of, source, student_live)


def per_device(teacher_rows, student_rows, teacher_head, student_head, lengths, owner):
    groups = lax.axis_size("grp")
    seq_count = teacher_rows.shape[0]
    positions = teacher_rows.shape[1]
    slot_count = seq_count * positions
    pad_rows = student_rows.shape[1]
    own_group = lax.axis_index("grp")
    teacher_of, source, student_live = routing_tables(
        lengths, owner, groups, seq_count, positions, pad_rows
    )
    local_teacher = teacher_rows.reshape(slot_count, teacher_rows.shape[2])
    local_student = student_rows.reshape(pad_rows, student_rows.shape[2])
    own_source = lax.dynamic_index_in_dim(source, own_group, 0, keepdims=False)
    sent_teacher = jnp.take(local_teacher, own_source, axis=0)
    row_position = teacher_of[:, None] * pad_rows + jnp.arange(pad_rows, dtype=jnp.int32)[None, :]
    teacher_full, student_full = (
        lax.all_gather(sent_teacher, "vocab", axis=1, tiled=True),
        lax.all_gather(local_student, "vocab", axis=1, tiled=True),
    )
    raw_teacher = jnp.dot(
        lax.all_gather(teacher_full, "grp", axis=0, tiled=True),
        teacher_head,
        preferred_element_type=jnp.float32,
    )
    student_logits = jnp.dot(
        lax.all_gather(student_full, "grp", axis=0, tiled=True),
        student_head,
        preferred_element_type=jnp.float32,
    )
    teacher_logits = jnp.take(raw_teacher, row_position.reshape(-1), axis=0)
    weight = student_live.reshape(-1).astype(jnp.float32)
    teacher_top, student_top = lax.pmax(
        (jnp.max(teacher_logits, axis=1), jnp.max(student_logits, axis=1)), ("grp", "vocab")
    )
    teacher_total, student_total = lax.psum(
        (
            jnp.sum(jnp.exp(teacher_logits - teacher_top[:, None]), axis=1),
            jnp.sum(jnp.exp(student_logits - student_top[:, None]), axis=1),
        ),
        ("grp", "vocab"),
    )
    teacher_lse = teacher_top + jnp.log(teacher_total)
    student_lse = student_top + jnp.log(student_total)
    log_q = student_logits - student_lse[:, None]
    log_p = teacher_logits - teacher_lse[:, None]
    student_prob = jnp.exp(log_q)
    log_ratio = log_q - log_p
    kl_rows = lax.psum(jnp.sum(student_prob * log_ratio, axis=1), ("grp", "vocab"))
    kl_rows = kl_rows * weight
    grad_logits = (weight[:, None] * student_prob * (log_ratio - kl_rows[:, None])).astype(
        jnp.bfloat16
    )
    partial_value = jnp.einsum(
        "rv,dv->rd", grad_logits, student_head, preferred_element_type=jnp.float32
    )
    feature_totals_acc = lax.psum_scatter(
        partial_value.astype(jnp.bfloat16), "vocab", scatter_dimension=1, tiled=True
    )
    grad_rows = lax.psum_scatter(feature_totals_acc, "grp", scatter_dimension=0, tiled=True)
    divergence = lax.dynamic_slice_in_dim(kl_rows, own_group * pad_rows, pad_rows, 0)
    return (divergence.reshape(1, pad_rows), grad_rows.reshape(1, pad_rows, grad_rows.shape[1]))


def solution(mesh):
    placed = (
        P("grp", None, "vocab"),
        P("grp", None, "vocab"),
        P(None, ("grp", "vocab")),
        P(None, ("grp", "vocab")),
        P(),
        P(),
    )
    return jax.shard_map(
        per_device,
        mesh=mesh,
        in_specs=placed,
        out_specs=(P("grp", None), P("grp", None, "vocab")),
        check_vma=False,
    )
```

profile of v0, /device:TPU:0, one launch (start us, length us, event | category | flops | bytes accessed | tf_op | source)
XLA Modules:
  0.0 356.8 jit_solution(3793422730505756832)
XLA Ops:
  7.2 0.9 reshape.194
  8.1 0.1 lt.122
  8.3 0.1 lt.125
  8.4 0.2 reduce_window_sum.11
  8.6 0.2 select_reduce_fusion.1
  8.9 1.6 gather_fusion.1
  10.5 0.1 broadcast_select_fusion
  10.5 7.7 %all_gather.14 = bf16[32,4096]{1,0:T(8,128)(2,1)} all-gather(bf16[32,1024]{1,0:T(8,128)(2,1)S(1)} %broadcast_select_fusion), channel_id=1, replica_groups=mesh['grp'=8,'vocab'=4] {'vocab'}, dimensions={1}, use_global_device_ids=true | all-gather | bytes 327680 | tf_op jit(solution)/shard_map/all_gather | solution.py:47
  18.3 8.2 %all-gather = bf16[1,32,5120]{2,1,0:T(8,128)(2,1)} all-gather(bf16[1,32,1280]{2,1,0:T(8,128)(2,1)} %param.7), channel_id=2, replica_groups=mesh['grp'=8,'vocab'=4] {'vocab'}, dimensions={2}, use_global_device_ids=true | all-gather | bytes 409600 | tf_op jit(solution)/shard_map/all_gather | solution.py:48
  26.6 0.1 reduce_sum.57
  26.7 0.7 reshape.193
  27.4 0.1 slice_reduce_fusion
  27.5 0.1 select_reduce_fusion.2
  27.7 0.6 gather_fusion
  28.4 0.1 add.134
  28.5 0.1 add.126
  28.6 0.1 lt.118
  28.8 40.1 %all-gather.5.cloned.1.call-done = bf16[256,4096]{1,0:T(8,128)(2,1)} async-done(((bf16[32,4096]{1,0:T(8,128)(2,1)}), bf16[256,4096]{1,0:T(8,128)(2,1)}) %all-gather.5.cloned.1.call-update) | async-done | bytes 2097168 | tf_op jit(solution)/shard_map/all_gather | solution.py:51
  68.9 2.9 fusion.13
  71.8 1.0 gather_fusion.2
  72.8 0.1 copy.10
  73.0 51.0 %all-gather.7.cloned.1.call-done = bf16[1,256,5120]{2,1,0:T(8,128)(2,1)} async-done(((bf16[1,32,5120]{2,1,0:T(8,128)(2,1)}), bf16[1,256,5120]{2,1,0:T(8,128)(2,1)}) %all-gather.7.cloned.1.call-update) | async-done | bytes 2621456 | tf_op jit(solution)/shard_map/all_gather | solution.py:56
  124.0 2.9 fusion.12
  126.9 39.3 %all-reduce.1 = (f32[256]{0:T(256)S(1)}, f32[256]{0:T(256)S(1)}) all-reduce(f32[256]{0:T(256)S(1)} %select_reduce_fusion, f32[256]{0:T(256)S(1)} %get-tuple-element.10), channel_id=1, replica_groups=mesh['grp'=8,'vocab'=4] {'grp','vocab'}, use_global_device_ids=true, to_apply=%region_9.10 | all-reduce | flops 512 | bytes 4096 | tf_op jit(solution)/shard_map/pmax | solution.py:62
  166.2 0.1 exponential_reduce_fusion
  166.3 39.9 %all-reduce = (f32[256]{0:T(256)S(1)}, f32[256]{0:T(256)S(1)}) all-reduce(f32[256]{0:T(256)S(1)} %get-tuple-element.12, f32[256]{0:T(256)S(1)} %get-tuple-element.13), channel_id=1, replica_groups=mesh['grp'=8,'vocab'=4] {'grp','vocab'}, use_global_device_ids=true, to_apply=%region_11.12 | all-reduce | flops 512 | bytes 4096 | tf_op jit(solution)/shard_map/psum | solution.py:65
  206.2 0.1 multiply_reduce_fusion
  206.3 40.1 %psum.23 = f32[256]{0:T(256)S(1)} all-reduce(f32[256]{0:T(256)S(1)} %multiply_reduce_fusion), channel_id=1, replica_groups=mesh['grp'=8,'vocab'=4] {'grp','vocab'}, use_global_device_ids=true, to_apply=%region_13.14 | all-reduce | flops 256 | bytes 2048 | tf_op jit(solution)/shard_map/psum | solution.py:78
  246.4 2.4 convolution_convert_fusion
  248.9 34.8 %reduce-scatter.3.cloned.1.call-done = bf16[256,1280]{1,0:T(8,128)(2,1)} async-done(((bf16[256,5120]{1,0:T(8,128)(2,1)}), bf16[256,1280]{1,0:T(8,128)(2,1)}) %reduce-scatter.3.cloned.1.call-update) | async-done | bytes 655376 | tf_op jit(solution)/shard_map/reduce_scatter | solution.py:86
  283.7 0.6 dynamic-slice_bitcast_fusion
  284.3 65.9 %reduce-scatter.5.cloned.1.call-done = bf16[32,1280]{1,0:T(8,128)(2,1)} async-done(((bf16[256,1280]{1,0:T(8,128)(2,1)}), bf16[32,1280]{1,0:T(8,128)(2,1)}) %reduce-scatter.5.cloned.1.call-update) | async-done | bytes 81936 | tf_op jit(solution)/shard_map/reduce_scatter | solution.py:89
  (30 shorter events, 0.6 us)
Async XLA Ops:
  7.2 116.9 %copy-start = (bf16[5120,256]{1,0:T(8,128)(2,1)S(1)}, bf16[5120,256]{1,0:T(8,128)(2,1)}, u32[]{:S(2)}) copy-start(bf16[5120,256]{1,0:T(8,128)(2,1)} %param.9) | copy-start | bytes 7864324
  7.2 61.7 %all-gather.5.cloned.1.call-start = ((), (), s32[]{:S(2)}) async-start(), calls=%async_computation.2 | async-start | bytes 2359296 | tf_op jit(solution)/shard_map/all_gather | solution.py:51
  18.3 105.8 %all-gather.7.cloned.1.call-start = ((), (), s32[]{:S(2)}) async-start(), calls=%async_computation.5 | async-start | bytes 2949120 | tf_op jit(solution)/shard_map/all_gather | solution.py:56
  26.5 257.2 %reduce-scatter.3.cloned.1.call-start = ((), (), s32[]{:S(2)}) async-start(), calls=%async_computation.3 | async-start | bytes 3276800 | tf_op jit(solution)/shard_map/reduce_scatter | solution.py:86
  248.9 101.4 %reduce-scatter.5.cloned.1.call-start = ((), (), s32[]{:S(2)}) async-start(), calls=%async_computation.4 | async-start | bytes 737280 | tf_op jit(solution)/shard_map/reduce_scatter | solution.py:89
Sparse Core Ops, SparseCore 0:
  18.4 50.4 all-gather.4
  71.0 52.9 all-gather.6
  249.0 34.6 reduce-scatter.2
  287.4 62.7 reduce-scatter.4
where the time goes:
time: 357 us
  waiting for transfers between devices  192 us (54%)
  blocking collectives  135 us (38%)
  between operations  13.9 us (4%)
  matrix products  8.25 us (2%)
  local copies, waits for them, and re-layouts  6.15 us (2%)
    reduce_scatter x1, waiting for transfers between devices, per_device(): lax.psum_scatter(feature_totals_acc, 'grp', scatter_dimension=0, tiled=True)  65.9 us
    all_gather x1, waiting for transfers between devices, per_device(): lax.all_gather(student_full, 'grp', axis=0, tiled=True)  51 us
    psum x1, blocking collectives, per_device(): lax.psum(jnp.sum(student_prob * log_ratio, axis=1), ('grp', 'vocab'))  40.1 us
    all_gather x1, waiting for transfers between devices, per_device(): lax.all_gather(teacher_full, 'grp', axis=0, tiled=True)  40.1 us
    psum x1, blocking collectives, per_device(): lax.psum((jnp.sum(jnp.exp(teacher_logits - teacher_top[:, None]), axis=1)...  39.9 us
    pmax x1, blocking collectives, per_device(): lax.pmax((jnp.max(teacher_logits, axis=1), jnp.max(student_logits, axis=1...  39.3 us
    reduce_scatter x1, waiting for transfers between devices, per_device(): lax.psum_scatter(partial_value.astype(jnp.bfloat16), 'vocab', scatter_dim...  34.8 us
    all_gather x1, blocking collectives, per_device(): lax.all_gather(local_student, 'vocab', axis=1, tiled=True)  8.2 us
  transfers between devices with their start and end apart: 4, of which 4 were waited for; matrix products, arithmetic and copies ran while one was open for 2% of the time, Pallas kernels for 0%

commit v1 on v0

--- a/solution.py
+++ b/solution.py
@@ -63,11 +63,14 @@
         (jnp.max(teacher_logits, axis=1), jnp.max(student_logits, axis=1)), ("grp", "vocab")
     )
     teacher_total, student_total = lax.psum(
-        (
-            jnp.sum(jnp.exp(teacher_logits - teacher_top[:, None]), axis=1),
-            jnp.sum(jnp.exp(student_logits - student_top[:, None]), axis=1),
+        lax.psum(
+            (
+                jnp.sum(jnp.exp(teacher_logits - teacher_top[:, None]), axis=1),
+                jnp.sum(jnp.exp(student_logits - student_top[:, None]), axis=1),
+            ),
+            "vocab",
         ),
-        ("grp", "vocab"),
+        "grp",
     )
     teacher_lse = teacher_top + jnp.log(teacher_total)
     student_lse = student_top + jnp.log(student_total)

time: 357 us -> 342 us (0.958)
  blocking collectives: 135 us -> 118 us
    psum x1, blocking collectives: 39.9 us -> 6.56 us  [per_device(): lax.psum((jnp.sum(jnp.exp(teacher_logits - teacher_top[:, None]), axis=1)...]
    psum x0 -> x1, blocking collectives: none -> 19.8 us  [per_device(): lax.psum(lax.psum((jnp.sum(jnp.exp(teacher_logits - teacher_top[:, None])...]
where the time goes in v1:
time: 342 us; the launch traced here: 341 us
  waiting for transfers between devices  193 us (56%)
  blocking collectives  118 us (35%)
  between operations  13.9 us (4%)
  matrix products  8.25 us (2%)
  local copies, waits for them, and re-layouts  6.15 us (2%)
    reduce_scatter x1, waiting for transfers between devices, per_device(): lax.psum_scatter(feature_totals_acc, 'grp', scatter_dimension=0, tiled=True)  65.9 us
    all_gather x1, waiting for transfers between devices, per_device(): lax.all_gather(student_full, 'grp', axis=0, tiled=True)  51 us
    all_gather x1, waiting for transfers between devices, per_device(): lax.all_gather(teacher_full, 'grp', axis=0, tiled=True)  40.1 us
    pmax x1, blocking collectives, per_device(): lax.pmax((jnp.max(teacher_logits, axis=1), jnp.max(student_logits, axis=1...  39.2 us
    psum x1, blocking collectives, per_device(): lax.psum(jnp.sum(student_prob * log_ratio, axis=1), ('grp', 'vocab'))  36.9 us
    reduce_scatter x1, waiting for transfers between devices, per_device(): lax.psum_scatter(partial_value.astype(jnp.bfloat16), 'vocab', scatter_dim...  36 us
    psum x1, blocking collectives, per_device(): lax.psum(lax.psum((jnp.sum(jnp.exp(teacher_logits - teacher_top[:, None])...  19.8 us
    all_gather x1, blocking collectives, per_device(): lax.all_gather(local_student, 'vocab', axis=1, tiled=True)  8.2 us
  transfers between devices with their start and end apart: 4, of which 4 were waited for; matrix products, arithmetic and copies ran while one was open for 2% of the time, Pallas kernels for 0%

profile of v1, /device:TPU:0, one launch (start us, length us, event | category | flops | bytes accessed | tf_op | source)
XLA Modules:
  0.0 341.2 jit_solution(1030487217995873523)
XLA Ops:
  7.2 0.9 reshape.194
  8.1 0.1 lt.122
  8.3 0.1 lt.125
  8.4 0.2 reduce_window_sum.11
  8.6 0.2 select_reduce_fusion.1
  8.9 1.6 gather_fusion.1
  10.5 0.1 broadcast_select_fusion
  10.5 7.7 %all_gather.14 = bf16[32,4096]{1,0:T(8,128)(2,1)} all-gather(bf16[32,1024]{1,0:T(8,128)(2,1)S(1)} %broadcast_select_fusion), channel_id=1, replica_groups=mesh['grp'=8,'vocab'=4] {'vocab'}, dimensions={1}, use_global_device_ids=true | all-gather | bytes 327680 | tf_op jit(solution)/shard_map/all_gather | solution.py:47
  18.3 8.2 %all-gather = bf16[1,32,5120]{2,1,0:T(8,128)(2,1)} all-gather(bf16[1,32,1280]{2,1,0:T(8,128)(2,1)} %param.7), channel_id=2, replica_groups=mesh['grp'=8,'vocab'=4] {'vocab'}, dimensions={2}, use_global_device_ids=true | all-gather | bytes 409600 | tf_op jit(solution)/shard_map/all_gather | solution.py:48
  26.6 0.1 reduce_sum.57
  26.7 0.7 reshape.193
  27.4 0.1 slice_reduce_fusion
  27.5 0.1 select_reduce_fusion.2
  27.7 0.6 gather_fusion
  28.4 0.1 add.138
  28.6 0.1 lt.118
  28.8 40.1 %all-gather.5.cloned.1.call-done = bf16[256,4096]{1,0:T(8,128)(2,1)} async-done(((bf16[32,4096]{1,0:T(8,128)(2,1)}), bf16[256,4096]{1,0:T(8,128)(2,1)}) %all-gather.5.cloned.1.call-update) | async-done | bytes 2097168 | tf_op jit(solution)/shard_map/all_gather | solution.py:51
  68.9 2.9 fusion.13
  71.8 1.0 gather_fusion.2
  72.8 0.1 copy.10
  73.0 51.0 %all-gather.7.cloned.1.call-done = bf16[1,256,5120]{2,1,0:T(8,128)(2,1)} async-done(((bf16[1,32,5120]{2,1,0:T(8,128)(2,1)}), bf16[1,256,5120]{2,1,0:T(8,128)(2,1)}) %all-gather.7.cloned.1.call-update) | async-done | bytes 2621456 | tf_op jit(solution)/shard_map/all_gather | solution.py:56
  124.0 2.9 fusion.12
  126.9 39.2 %all-reduce = (f32[256]{0:T(256)S(1)}, f32[256]{0:T(256)S(1)}) all-reduce(f32[256]{0:T(256)S(1)} %select_reduce_fusion, f32[256]{0:T(256)S(1)} %get-tuple-element.12), channel_id=1, replica_groups=mesh['grp'=8,'vocab'=4] {'grp','vocab'}, use_global_device_ids=true, to_apply=%region_10.11 | all-reduce | flops 512 | bytes 4096 | tf_op jit(solution)/shard_map/pmax | solution.py:62
  166.1 0.1 exponential_reduce_fusion
  166.2 6.6 %all-reduce.2 = (f32[256]{0:T(256)S(1)}, f32[256]{0:T(256)S(1)}) all-reduce(f32[256]{0:T(256)S(1)} %get-tuple-element.14, f32[256]{0:T(256)S(1)} %get-tuple-element.15), channel_id=1, replica_groups=mesh['grp'=8,'vocab'=4] {'vocab'}, use_global_device_ids=true, to_apply=%region_12.13 | all-reduce | flops 512 | bytes 4096 | tf_op jit(solution)/shard_map/psum | solution.py:66
  172.8 19.8 %all-reduce.1 = (f32[256]{0:T(256)S(1)}, f32[256]{0:T(256)S(1)}) all-reduce(f32[256]{0:T(256)S(1)} %get-tuple-element.6, f32[256]{0:T(256)S(1)} %get-tuple-element.7), channel_id=1, replica_groups=mesh['grp'=8,'vocab'=4] {'grp'}, use_global_device_ids=true, to_apply=%region_13.14 | all-reduce | flops 512 | bytes 4096 | tf_op jit(solution)/shard_map/psum | solution.py:65
  192.6 0.1 multiply_reduce_fusion
  192.7 36.9 %psum.39 = f32[256]{0:T(256)S(1)} all-reduce(f32[256]{0:T(256)S(1)} %multiply_reduce_fusion), channel_id=1, replica_groups=mesh['grp'=8,'vocab'=4] {'grp','vocab'}, use_global_device_ids=true, to_apply=%region_15.16 | all-reduce | flops 256 | bytes 2048 | tf_op jit(solution)/shard_map/psum | solution.py:81
  229.7 2.4 convolution_convert_fusion
  232.2 36.0 %reduce-scatter.3.cloned.1.call-done = bf16[256,1280]{1,0:T(8,128)(2,1)} async-done(((bf16[256,5120]{1,0:T(8,128)(2,1)}), bf16[256,1280]{1,0:T(8,128)(2,1)}) %reduce-scatter.3.cloned.1.call-update) | async-done | bytes 655376 | tf_op jit(solution)/shard_map/reduce_scatter | solution.py:89
  268.2 0.6 dynamic-slice_bitcast_fusion
  268.8 65.9 %reduce-scatter.5.cloned.1.call-done = bf16[32,1280]{1,0:T(8,128)(2,1)} async-done(((bf16[256,1280]{1,0:T(8,128)(2,1)}), bf16[32,1280]{1,0:T(8,128)(2,1)}) %reduce-scatter.5.cloned.1.call-update) | async-done | bytes 81936 | tf_op jit(solution)/shard_map/reduce_scatter | solution.py:92
  (31 shorter events, 0.7 us)
Async XLA Ops:
  7.2 116.9 %copy-start = (bf16[5120,256]{1,0:T(8,128)(2,1)S(1)}, bf16[5120,256]{1,0:T(8,128)(2,1)}, u32[]{:S(2)}) copy-start(bf16[5120,256]{1,0:T(8,128)(2,1)} %param.9) | copy-start | bytes 7864324
  7.2 61.7 %all-gather.5.cloned.1.call-start = ((), (), s32[]{:S(2)}) async-start(), calls=%async_computation.2 | async-start | bytes 2359296 | tf_op jit(solution)/shard_map/all_gather | solution.py:51
  18.3 105.8 %all-gather.7.cloned.1.call-start = ((), (), s32[]{:S(2)}) async-start(), calls=%async_computation.5 | async-start | bytes 2949120 | tf_op jit(solution)/shard_map/all_gather | solution.py:56
  26.5 241.7 %reduce-scatter.3.cloned.1.call-start = ((), (), s32[]{:S(2)}) async-start(), calls=%async_computation.3 | async-start | bytes 3276800 | tf_op jit(solution)/shard_map/reduce_scatter | solution.py:89
  232.1 102.5 %reduce-scatter.5.cloned.1.call-start = ((), (), s32[]{:S(2)}) async-start(), calls=%async_computation.4 | async-start | bytes 737280 | tf_op jit(solution)/shard_map/reduce_scatter | solution.py:92
Sparse Core Ops, SparseCore 0:
  18.4 50.4 all-gather.4
  71.0 52.9 all-gather.6
  232.3 35.8 reduce-scatter.2
  271.9 62.7 reduce-scatter.4
